TPU v7x, 32 devices: a whole 2x2x4 slice. The times are simulated.
32 devices in a mesh: tenant: 2 (over y), ctx: 2 (over x), head: 8 (over z, core).
Axes of the slice: x: 2, y: 2, z: 4, core: 2. Of those that a mesh axis runs over, the one named last changes fastest.
Arguments:
- tokens: bfloat16 [1024, 4608], P(('tenant', 'ctx'), 'head'), parts along dimension 0, may hold values from -6 to 6
- query_frozen_matrix: bfloat16 [4608, 2048], P('ctx', 'head'), may hold values from -0.09375 to 0.09375
- key_weight: bfloat16 [4608, 1024], P('ctx', 'head'), may hold values from -0.09375 to 0.09375
- value_frozen_matrix: bfloat16 [4608, 1024], P('ctx', 'head'), may hold values from -0.09375 to 0.09375
- query_down: bfloat16 [9216, 16], P('tenant'), parts along dimension 0, may hold values from -0.09375 to 0.09375
- query_adapter_expand: bfloat16 [32, 2048], P('tenant', 'head'), parts along dimension 0, may hold values from -1.5 to 1.5
- value_down: bfloat16 [9216, 16], P('tenant'), parts along dimension 0, may hold values from -0.09375 to 0.09375
- value_adapter_expand: bfloat16 [32, 1024], P('tenant', 'head'), parts along dimension 0, may hold values from -1.5 to 1.5
- block_order: int32 [8], P('tenant'), parts along dimension 0, may hold values from 0 to 3, each once
- doc_starts: int32 [24], P('tenant'), parts along dimension 0, may hold values from 0 to 511, as said below
- prompt_of: int32 [24], P('tenant'), parts along dimension 0, may hold values from 0 to 11, as said below
Outputs:
- attended: bfloat16 [1024, 2048], P(('tenant', 'ctx'), 'head'), parts along dimension 0
There are 2 independent parts, one for each index of `tenant`. A program takes and returns all parts, laid end to end along the dimension named above; an argument that names none is the same for every part. Nothing has to cross between parts.
Inputs may be any that keep to these rules, and one draw needn't show every extreme that they name: `doc_starts`: strictly increasing with first entry 0; the segments come in 4 groups of three: a prompt, a chosen and a rejected response. `prompt_of`: for segment j = 3k it is j; for j = 3k + 1 it is 3k; for j = 3k + 2 it is 3k or j. `block_order`: each of 0 to 3 once.
All inputs are finite; a program needn't handle non-finite values.
Results may differ from a plain program's by a relative error of at most 0.012.
Values may be sent and summed in bfloat16 or wider, within the bound.
No kernel may reach another device: no remote copies, remote signals or barrier semaphores. Data moves between devices by JAX's collectives and lax.ppermute only.
A program may use at most 64 MiB of HBM per device.

v0:
```python
import math
import jax
import jax.numpy as jnp
from jax import lax
from jax.sharding import PartitionSpec as P

HD = 128
softcap_limit = 50.0
query_scale = 144.0 ** (-0.5)
adapter_scaling = 2.0
rope_base = 10000.0


def row_meta(row_ids, block_order, doc_starts, prompt_of, block_len, sequence_len):
    block_count = block_order.shape[0]
    block_id = row_ids // block_len
    one_hot = block_id[:, None] == jnp.arange(block_count, dtype=jnp.int32)[None, :]
    ordered = jnp.sum(jnp.where(one_hot, block_order[None, :], 0), axis=1)
    places = ordered * block_len + row_ids % block_len
    segment = jnp.sum((doc_starts[None, :] <= places[:, None]).astype(jnp.int32), axis=1) - 1
    seg_ids = jnp.arange(doc_starts.shape[0], dtype=jnp.int32)
    selected = segment[:, None] == seg_ids[None, :]
    prompt_seg = jnp.sum(jnp.where(selected, prompt_of[None, :], 0), axis=1)
    own_start = jnp.sum(jnp.where(selected, doc_starts[None, :], 0), axis=1)
    next_starts = jnp.concatenate([doc_starts[1:], jnp.full((1,), sequence_len, jnp.int32)])
    prompt_sel = prompt_seg[:, None] == seg_ids[None, :]
    prompt_len = jnp.sum(jnp.where(prompt_sel, (next_starts - doc_starts)[None, :], 0), axis=1)
    rotary_pos = places - own_start + jnp.where(prompt_seg != segment, prompt_len, 0)
    return (places, segment, prompt_seg, rotary_pos)


def rotate(values_in, rotary_pos):
    width_half = values_in.shape[-1] // 2
    frequency = jnp.exp(
        jnp.arange(width_half, dtype=jnp.float32)
        * (-2.0 * math.log(rope_base) / values_in.shape[-1])
    )
    angles = rotary_pos.astype(jnp.float32)[:, None] * frequency[None, :]
    cosine = jnp.concatenate([jnp.cos(angles), jnp.cos(angles)], axis=-1)[:, None, :]
    sine_part = jnp.concatenate([jnp.sin(angles), jnp.sin(angles)], axis=-1)[:, None, :]
    rotated = jnp.concatenate([-values_in[..., width_half:], values_in[..., :width_half]], axis=-1)
    return values_in * cosine + rotated * sine_part


def visible_mask(query_info, key_info):
    same_doc = (key_info[1][None, :] == query_info[1][:, None]) & (
        key_info[0][None, :] <= query_info[0][:, None]
    )
    from_prompt = (key_info[1][None, :] == query_info[2][:, None]) & (
        query_info[2] != query_info[1]
    )[:, None]
    return same_doc | from_prompt


def local(
    tokens,
    query_frozen_matrix,
    key_weight,
    value_frozen_matrix,
    query_down,
    query_adapter_expand,
    value_down,
    value_adapter_expand,
    block_order,
    doc_starts,
    prompt_of,
):
    tok_rows = tokens.shape[0]
    cycle_size = lax.axis_size("ctx")
    device = lax.axis_index("ctx")
    sequence_len = tok_rows * cycle_size
    block_len = tok_rows // 2
    full_tokens = lax.all_gather(tokens, "head", axis=1, tiled=True)

    def add_rows(weight_part):
        return jnp.dot(full_tokens, weight_part, preferred_element_type=jnp.float32)

    frozen_query_output = add_rows(lax.all_gather(query_frozen_matrix, "ctx", axis=0, tiled=True))
    key_base = add_rows(lax.all_gather(key_weight, "ctx", axis=0, tiled=True))
    frozen_value_output = add_rows(lax.all_gather(value_frozen_matrix, "ctx", axis=0, tiled=True))
    own_ids = device * tok_rows + jnp.arange(tok_rows, dtype=jnp.int32)
    own_info = row_meta(own_ids, block_order, doc_starts, prompt_of, block_len, sequence_len)
    local_heads = query_frozen_matrix.shape[1] // HD
    local_kv = key_weight.shape[1] // HD
    per_kv = local_heads // local_kv
    query_adapter_hidden = jnp.dot(
        full_tokens, query_down, preferred_element_type=jnp.float32
    ).astype(jnp.bfloat16)
    query_states = frozen_query_output + adapter_scaling * jnp.dot(
        query_adapter_hidden, query_adapter_expand, preferred_element_type=jnp.float32
    )
    query_states = (
        rotate(query_states.reshape(tok_rows, local_heads, HD), own_info[3]) * query_scale
    ).astype(jnp.bfloat16)
    query_heads = query_states.reshape(tok_rows, local_kv, per_kv, HD)
    key_proj = (
        rotate(key_base.reshape(tok_rows, local_kv, HD), own_info[3])
        .astype(jnp.bfloat16)
        .reshape(tok_rows, local_kv * HD)
    )
    value_adapter_hidden = jnp.dot(
        full_tokens, value_down, preferred_element_type=jnp.float32
    ).astype(jnp.bfloat16)
    value_projected = (
        frozen_value_output
        + adapter_scaling
        * jnp.dot(value_adapter_hidden, value_adapter_expand, preferred_element_type=jnp.float32)
    ).astype(jnp.bfloat16)
    pieces = (
        lax.all_gather(key_proj, "ctx", axis=0, tiled=True),
        lax.all_gather(value_projected, "ctx", axis=0, tiled=True),
    )
    key_ids = jnp.arange(pieces[0].shape[0], dtype=jnp.int32)
    key_block = pieces[0]
    value_block = pieces[1]
    key_info = row_meta(key_ids, block_order, doc_starts, prompt_of, block_len, sequence_len)
    visible = visible_mask(own_info, key_info)
    key_heads = key_block.reshape(key_block.shape[0], local_kv, HD)
    value_heads = value_block.reshape(value_block.shape[0], local_kv, HD)
    scores = jnp.einsum(
        "tkgd,skd->kgts", query_heads, key_heads, preferred_element_type=jnp.float32
    )
    capped = softcap_limit * jnp.tanh(scores / softcap_limit)
    unnorm = jnp.where(visible[None, None], jnp.exp(capped), jnp.zeros_like(capped))
    denominator = jnp.sum(unnorm, axis=-1)
    numerator = jnp.einsum(
        "kgts,skd->tkgd",
        unnorm.astype(jnp.bfloat16),
        value_heads,
        preferred_element_type=jnp.float32,
    )
    numerator, denominator = (numerator, denominator)
    attended = numerator / jnp.transpose(denominator, (2, 0, 1))[..., None]
    return attended.reshape(tok_rows, local_heads * HD).astype(jnp.bfloat16)


def solution(mesh):
    in_specs = (
        P(("tenant", "ctx"), "head"),
        P("ctx", "head"),
        P("ctx", "head"),
        P("ctx", "head"),
        P("tenant", None),
        P("tenant", "head"),
        P("tenant", None),
        P("tenant", "head"),
        P("tenant"),
        P("tenant"),
        P("tenant"),
    )
    out_specs = P(("tenant", "ctx"), "head")
    return jax.shard_map(local, mesh=mesh, in_specs=in_specs, out_specs=out_specs, check_vma=False)
```

profile of v0, /device:TPU:0, one launch (start us, length us, event | category | flops | bytes accessed | tf_op | source)
XLA Modules:
  0.0 143.6 jit_solution(536576771758366168)
XLA Ops:
  6.5 0.0 all-gather.9.cloned.1.call-start
  6.6 0.7 all-gather.9.cloned.1.call-update
  7.3 0.0 all-gather.5.cloned.1.call-start
  7.3 0.7 all-gather.5.cloned.1.call-update
  8.0 0.0 all-gather.11.cloned.1.call-start
  8.1 0.7 all-gather.11.cloned.1.call-update
  8.8 0.0 all-gather.7.cloned.1.call-start
  8.8 0.5 all-gather.7.cloned.1.call-update
  9.4 0.1 slice.15
  9.5 0.1 select_reduce_fusion.4
  9.6 0.1 convert_reduce_fusion.1
  9.7 0.1 select_reduce_fusion.3
  9.7 0.1 convert_reduce_fusion
  9.8 0.1 add_subtract_fusion
  9.9 0.1 select_reduce_fusion.1
  10.0 0.1 select_reduce_fusion
  10.1 0.3 multiply_cosine_fusion
  10.4 0.2 and_or_fusion
  10.7 23.7 %all-gather.9.cloned.1.call-done = bf16[4608,128]{1,0:T(8,128)(2,1)} async-done(((bf16[2304,128]{1,0:T(8,128)(2,1)}), bf16[4608,128]{1,0:T(8,128)(2,1)}) %all-gather.9.cloned.1.call-update) | async-done | bytes 1179664 | tf_op jit(solution)/shard_map/all_gather | solution.py:79
  34.4 33.1 %all-gather.5.cloned.1.call-done = bf16[256,4608]{0,1:T(8,128)(2,1)} async-done(((bf16[256,576]{0,1:T(8,128)(2,1)}), bf16[256,4608]{0,1:T(8,128)(2,1)}) %all-gather.5.cloned.1.call-update) | async-done | bytes 2359312 | tf_op jit(solution)/shard_map/all_gather | solution.py:73
  67.5 2.7 %fusion.30 = f32[256,128]{0,1:T(8,128)S(1)} fusion(bf16[256,4608]{0,1:T(8,128)(2,1)} %all-gather.5.cloned.1.call-done, bf16[4608,128]{1,0:T(8,128)(2,1)} %all-gather.9.cloned.1.call-done), kind=kOutput, calls=%fused_computation.76 | convolution fusion | flops 301989888 | bytes 3670016 | tf_op jit(solution)/shard_map/dot_general | solution.py:76
  70.4 4.9 %all_gather.22 = bf16[512,128]{0,1:T(8,128)(2,1)S(1)} all-gather(bf16[256,128]{0,1:T(8,128)(2,1)S(1)} %get-tuple-element.13), channel_id=1, replica_groups=mesh['tenant'=2,'ctx'=2,'head'=8] {'ctx'}, dimensions={0}, use_global_device_ids=true | all-gather | bytes 196608 | tf_op jit(solution)/shard_map/all_gather | solution.py:110
  75.3 1.0 convolution_multiply_fusion.1
  76.3 28.1 %all-gather.11.cloned.1.call-done = bf16[4608,256]{1,0:T(8,128)(2,1)} async-done(((bf16[2304,256]{1,0:T(8,128)(2,1)}), bf16[4608,256]{1,0:T(8,128)(2,1)}) %all-gather.11.cloned.1.call-update) | async-done | bytes 2359312 | tf_op jit(solution)/shard_map/all_gather | solution.py:78
  104.4 2.7 %convolution_add_fusion = f32[256,256]{0,1:T(8,128)S(1)} fusion(f32[256,256]{0,1:T(8,128)S(1)} %convolution_multiply_fusion.1, bf16[256,4608]{0,1:T(8,128)(2,1)S(1)} %copy-done.4, bf16[4608,256]{1,0:T(8,128)(2,1)} %all-gather.11.cloned.1.call-done), kind=kOutput, calls=%fused_computation.7 | convolution fusion | flops 604045312 | bytes 5242880 | tf_op jit(solution)/shard_map/dot_general | solution.py:76
  107.1 2.5 %convolution_multiply_fusion.2 = f32[256,128]{0,1:T(8,128)} fusion(bf16[16,128]{1,0:T(8,128)(2,1)} %param.18, bf16[256,4608]{0,1:T(8,128)(2,1)S(1)} %copy-done.4, bf16[4608,16]{0,1:T(8,128)(2,1)} %param.17), kind=kOutput, calls=%fused_computation.10 | convolution fusion | flops 38834176 | bytes 2641920 | tf_op jit(solution)/shard_map/dot_general | solution.py:107
  109.7 18.9 %all-gather.7.cloned.1.call-done = bf16[4608,128]{1,0:T(8,128)(2,1)} async-done(((bf16[2304,128]{1,0:T(8,128)(2,1)}), bf16[4608,128]{1,0:T(8,128)(2,1)}) %all-gather.7.cloned.1.call-update) | async-done | bytes 1179664 | tf_op jit(solution)/shard_map/all_gather | solution.py:80
  128.6 1.9 %fusion.5 = bf16[256,128]{0,1:T(8,128)(2,1)S(1)} fusion(f32[256,128]{0,1:T(8,128)} %convolution_multiply_fusion.2, bf16[256,4608]{0,1:T(8,128)(2,1)S(1)} %copy-done.4, bf16[4608,128]{1,0:T(8,128)(2,1)} %all-gather.7.cloned.1.call-done), kind=kOutput, calls=%fused_computation.11 | convolution fusion | flops 302055424 | bytes 3735552 | tf_op jit(solution)/shard_map/dot_general | solution.py:76
  130.5 4.9 %all_gather.20 = bf16[512,128]{0,1:T(8,128)(2,1)S(1)} all-gather(bf16[256,128]{0,1:T(8,128)(2,1)S(1)} %fusion.5), channel_id=1, replica_groups=mesh['tenant'=2,'ctx'=2,'head'=8] {'ctx'}, dimensions={0}, use_global_device_ids=true | all-gather | bytes 196608 | tf_op jit(solution)/shard_map/all_gather | solution.py:111
  135.5 0.5 fusion.29
  136.0 0.2 fusion.7
  136.3 0.8 copy.19
  (25 shorter events, 0.2 us)
Async XLA Ops:
  6.5 68.8 %copy-start = (bf16[4608,16]{0,1:T(8,128)(2,1)S(1)}, bf16[4608,16]{0,1:T(8,128)(2,1)}, u32[]{:S(2)}) copy-start(bf16[4608,16]{0,1:T(8,128)(2,1)} %param.15) | copy-start | bytes 442372
  6.5 2.8 %copy-start.1 = (s32[12]{0:T(128)S(1)}, s32[12]{0:T(128)}, u32[]{:S(2)}) copy-start(s32[12]{0:T(128)} %param.20) | copy-start | bytes 148
  6.5 2.9 %copy-start.2 = (s32[4]{0:T(128)S(1)}, s32[4]{0:T(128)}, u32[]{:S(2)}) copy-start(s32[4]{0:T(128)} %param.19) | copy-start | bytes 52
  6.5 3.4 %copy-start.3 = (s32[12]{0:T(128)S(1)}, s32[12]{0:T(128)}, u32[]{:S(2)}) copy-start(s32[12]{0:T(128)} %param.21) | copy-start | bytes 148
  6.5 27.9 %all-gather.9.cloned.1.call-start = ((), (), s32[]{:S(2)}) async-start(), calls=%async_computation.2 | async-start | bytes 1769472 | tf_op jit(solution)/shard_map/all_gather | solution.py:79
  7.3 60.3 %all-gather.5.cloned.1.call-start = ((), (), s32[]{:S(2)}) async-start(), calls=%async_computation | async-start | bytes 2654208 | tf_op jit(solution)/shard_map/all_gather | solution.py:73
  8.0 96.4 %all-gather.11.cloned.1.call-start = ((), (), s32[]{:S(2)}) async-start(), calls=%async_computation.3 | async-start | bytes 3538944 | tf_op jit(solution)/shard_map/all_gather | solution.py:78
  8.8 119.8 %all-gather.7.cloned.1.call-start = ((), (), s32[]{:S(2)}) async-start(), calls=%async_computation.1 | async-start | bytes 1769472 | tf_op jit(solution)/shard_map/all_gather | solution.py:80
  10.7 64.6 %copy-start.5 = (bf16[16,256]{1,0:T(8,128)(2,1)S(1)}, bf16[16,256]{1,0:T(8,128)(2,1)}, u32[]{:S(2)}) copy-start(bf16[16,256]{1,0:T(8,128)(2,1)} %param.16) | copy-start | bytes 24580
  67.5 7.8 %copy-start.4 = (bf16[256,4608]{0,1:T(8,128)(2,1)S(1)}, bf16[256,4608]{0,1:T(8,128)(2,1)}, u32[]{:S(2)}) copy-start(bf16[256,4608]{0,1:T(8,128)(2,1)} %all-gather.5.cloned.1.call-done) | copy-start | bytes 7077892
Sparse Core Ops, SparseCore 0:
  8.9 25.4 all-gather.8
  36.1 31.4 all-gather.4
  69.1 35.2 all-gather.10
  105.8 22.7 all-gather.6
where the time goes:
time: 144 us
  waiting for transfers between devices  106 us (74%)
  between operations  13.3 us (9%)
  matrix products  11.6 us (8%)
  blocking collectives  9.87 us (7%)
    all_gather x1, waiting for transfers between devices, local(): full_tokens = lax.all_gather(tokens, 'head', axis=1, tiled=True)  33.1 us
    all_gather x1, waiting for transfers between devices, local(): lax.all_gather(query_frozen_matrix, 'ctx', axis=0, tiled=True)  28.1 us
    all_gather x1, waiting for transfers between devices, local(): key_base = add_rows(lax.all_gather(key_weight, 'ctx', axis=0, tiled=True))  23.7 us
    all_gather x1, waiting for transfers between devices, local(): lax.all_gather(value_frozen_matrix, 'ctx', axis=0, tiled=True)  18.9 us
    dot_general x3, matrix products, add_rows(): return jnp.dot(full_tokens, weight_part, preferred_element_type=jnp.float32)  7.33 us
    all_gather x1, blocking collectives, local(): lax.all_gather(key_proj, 'ctx', axis=0, tiled=True)  4.93 us
    all_gather x1, blocking collectives, local(): lax.all_gather(value_projected, 'ctx', axis=0, tiled=True)  4.93 us
  transfers between devices with their start and end apart: 4, of which 4 were waited for; matrix products, arithmetic and copies ran while one was open for 7% of the time, Pallas kernels for 0%

commit v1 on v0

--- a/solution.py
+++ b/solution.py
@@ -1,14 +1,38 @@
+import functools
 import math
 import jax
 import jax.numpy as jnp
 from jax import lax
 from jax.sharding import PartitionSpec as P
+from jax.lax import axis_index, axis_size, ppermute
 
 HD = 128
 softcap_limit = 50.0
 query_scale = 144.0 ** (-0.5)
 adapter_scaling = 2.0
 rope_base = 10000.0
+
+
+def find_the_trails(mine_x, which_dim):
+    mine_x = jnp.moveaxis(mine_x, 0, which_dim)
+    y1 = mine_x.shape
+    return mine_x.reshape(*y1[:which_dim], y1[which_dim] * y1[which_dim + 1], *y1[which_dim + 2 :])
+
+
+def track_spot(xs, axis_name, pos_dim):
+    lanes = axis_size(axis_name)
+    grid = tuple(((nth, (nth + 1) % lanes) for nth in range(lanes)))
+    store = [xs]
+    while len(store) < lanes:
+        row_out = ppermute(store[-1], axis_name=axis_name, perm=grid)
+        store.append(row_out)
+    top = axis_index(axis_name)
+    y = jnp.stack(store)
+    store = y[(top - jnp.arange(lanes)) % lanes]
+    return find_the_trails(store, pos_dim)
+
+
+spread_the_stocks = functools.partial(track_spot, axis_name="head", pos_dim=1)
 
 
 def row_meta(row_ids, block_order, doc_starts, prompt_of, block_len, sequence_len):
@@ -70,7 +94,7 @@
     device = lax.axis_index("ctx")
     sequence_len = tok_rows * cycle_size
     block_len = tok_rows // 2
-    full_tokens = lax.all_gather(tokens, "head", axis=1, tiled=True)
+    full_tokens = spread_the_stocks(tokens)
 
     def add_rows(weight_part):
         return jnp.dot(full_tokens, weight_part, preferred_element_type=jnp.float32)

time: 144 us -> 110 us (0.76)
  waiting for transfers between devices: 106 us -> 66.4 us
  blocking collectives: 9.87 us -> 13.3 us
  local copies, waits for them, and re-layouts: 0.86 us -> 3.15 us
    ppermute x0 -> x7, waiting for transfers between devices: none -> 54.6 us  [track_spot(): row_out = ppermute(store[-1], axis_name=axis_name, perm=grid)]
    all_gather x1 -> x0, waiting for transfers between devices: 33.1 us -> none  [local(): full_tokens = lax.all_gather(tokens, 'head', axis=1, tiled=True)]
    all_gather x1, waiting for transfers between devices: 23.7 us -> 0.01 us  [local(): key_base = add_rows(lax.all_gather(key_weight, 'ctx', axis=0, tiled=True))]
    all_gather x1, waiting for transfers between devices: 18.9 us -> 0.02 us  [local(): lax.all_gather(value_frozen_matrix, 'ctx', axis=0, tiled=True)]
    all_gather x1, waiting for transfers between devices: 28.1 us -> 10.3 us  [local(): lax.all_gather(query_frozen_matrix, 'ctx', axis=0, tiled=True)]
    gather x0 -> x1, local copies, waits for them, and re-layouts: none -> 2.12 us  [track_spot(): store = y[(top - jnp.arange(lanes)) % lanes]]
    all_gather x1, blocking collectives: 4.93 us -> 6.87 us  [local(): lax.all_gather(key_proj, 'ctx', axis=0, tiled=True)]
    dot_general x1, matrix products: 2.53 us -> 0.96 us  [local(): jnp.dot(value_adapter_hidden, value_adapter_expand, preferred_element_typ...]
  transfers between devices with their start and end apart: 4 -> 10, of which waited for: 4 -> 8; matrix products, arithmetic and copies ran while one was open for 7% -> 10% of each run, Pallas kernels for 0% -> 0%
where the time goes in v1:
time: 110 us; the launch traced here: 109 us
  waiting for transfers between devices  66.4 us (60%)
  blocking collectives  13.3 us (12%)
  between operations  13.3 us (12%)
  matrix products  11.1 us (10%)
  local copies, waits for them, and re-layouts  3.15 us (3%)
  other arithmetic  1.39 us (1%)
    ppermute x7, waiting for transfers between devices, track_spot(): row_out = ppermute(store[-1], axis_name=axis_name, perm=grid)  54.6 us
    all_gather x1, waiting for transfers between devices, local(): lax.all_gather(query_frozen_matrix, 'ctx', axis=0, tiled=True)  10.3 us
    dot_general x3, matrix products, add_rows(): return jnp.dot(full_tokens, weight_part, preferred_element_type=jnp.float32)  7.68 us
    all_gather x1, blocking collectives, local(): lax.all_gather(key_proj, 'ctx', axis=0, tiled=True)  6.87 us
    all_gather x1, blocking collectives, local(): lax.all_gather(value_projected, 'ctx', axis=0, tiled=True)  6.46 us
  transfers between devices with their start and end apart: 10, of which 8 were waited for; matrix products, arithmetic and copies ran while one was open for 10% of the time, Pallas kernels for 0%

profile of v1, /device:TPU:0, one launch (start us, length us, event | category | flops | bytes accessed | tf_op | source)
XLA Modules:
  0.0 109.4 jit_solution(7638920419863888257)
XLA Ops:
  6.6 0.7 all-gather.6.cloned.1.call-update
  7.3 0.7 all-gather.4.cloned.1.call-update
  8.1 0.5 collective-permute-start
  8.6 0.1 all-gather.8.cloned.1.call-update
  8.9 0.1 select_reduce_fusion.4
  9.0 0.1 convert_reduce_fusion.1
  9.1 0.1 select_reduce_fusion.3
  9.2 0.1 convert_reduce_fusion
  9.3 0.1 add_subtract_fusion
  9.3 0.1 select_reduce_fusion.1
  9.4 0.1 select_reduce_fusion
  9.5 7.7 %collective-permute-done = bf16[256,576]{0,1:T(8,128)(2,1)S(1)} collective-permute-done((bf16[256,576]{0,1:T(8,128)(2,1)}, bf16[256,576]{0,1:T(8,128)(2,1)S(1)}, u32[]{:S(2)}, u32[]{:S(2)}) %collective-permute-start) | collective-permute-done | bytes 294944 | tf_op jit(solution)/shard_map/ppermute | solution.py:27
  17.3 0.3 multiply_cosine_fusion
  17.6 7.6 %collective-permute-done.1 = bf16[256,576]{0,1:T(8,128)(2,1)S(1)} collective-permute-done((bf16[256,576]{0,1:T(8,128)(2,1)S(1)}, bf16[256,576]{0,1:T(8,128)(2,1)S(1)}, u32[]{:S(2)}, u32[]{:S(2)}) %collective-permute-start.1) | collective-permute-done | bytes 294944 | tf_op jit(solution)/shard_map/ppermute | solution.py:27
  25.2 0.2 and_or_fusion
  25.5 7.7 %collective-permute-done.2 = bf16[256,576]{0,1:T(8,128)(2,1)S(1)} collective-permute-done((bf16[256,576]{0,1:T(8,128)(2,1)S(1)}, bf16[256,576]{0,1:T(8,128)(2,1)S(1)}, u32[]{:S(2)}, u32[]{:S(2)}) %collective-permute-start.2) | collective-permute-done | bytes 294944 | tf_op jit(solution)/shard_map/ppermute | solution.py:27
  33.2 7.9 %collective-permute-done.3 = bf16[256,576]{0,1:T(8,128)(2,1)S(1)} collective-permute-done((bf16[256,576]{0,1:T(8,128)(2,1)S(1)}, bf16[256,576]{0,1:T(8,128)(2,1)S(1)}, u32[]{:S(2)}, u32[]{:S(2)}) %collective-permute-start.3) | collective-permute-done | bytes 294944 | tf_op jit(solution)/shard_map/ppermute | solution.py:27
  41.2 7.9 %collective-permute-done.4 = bf16[256,576]{0,1:T(8,128)(2,1)S(1)} collective-permute-done((bf16[256,576]{0,1:T(8,128)(2,1)S(1)}, bf16[256,576]{0,1:T(8,128)(2,1)S(1)}, u32[]{:S(2)}, u32[]{:S(2)}) %collective-permute-start.4) | collective-permute-done | bytes 294944 | tf_op jit(solution)/shard_map/ppermute | solution.py:27
  49.1 7.9 %collective-permute-done.5 = bf16[256,576]{0,1:T(8,128)(2,1)S(1)} collective-permute-done((bf16[256,576]{0,1:T(8,128)(2,1)S(1)}, bf16[256,576]{0,1:T(8,128)(2,1)S(1)}, u32[]{:S(2)}, u32[]{:S(2)}) %collective-permute-start.5) | collective-permute-done | bytes 294944 | tf_op jit(solution)/shard_map/ppermute | solution.py:27
  57.1 7.9 %collective-permute-done.6 = bf16[256,576]{0,1:T(8,128)(2,1)S(1)} collective-permute-done((bf16[256,576]{0,1:T(8,128)(2,1)S(1)}, bf16[256,576]{0,1:T(8,128)(2,1)S(1)}, u32[]{:S(2)}, u32[]{:S(2)}) %collective-permute-start.6) | collective-permute-done | bytes 294944 | tf_op jit(solution)/shard_map/ppermute | solution.py:27
  65.0 2.1 %gather_fusion = bf16[8,256,576]{1,2,0:T(8,128)(2,1)} fusion(bf16[8,256,576]{1,2,0:T(8,128)(2,1)S(1)} %bitcast_dynamic-update-slice_fusion, s32[1024]{0:T(1024)S(1)} %pad_clamp_fusion), kind=kCustom, calls=%fused_computation | custom fusion | bytes 4718624 | tf_op jit(solution)/shard_map/gather | solution.py:31
  67.1 3.0 %fusion.32 = f32[256,128]{0,1:T(8,128)S(1)} fusion(bf16[256,4608]{0,1:T(8,128)(2,1)} %bitcast.82, bf16[4608,128]{1,0:T(8,128)(2,1)} %all-gather.6.cloned.1.call-done), kind=kOutput, calls=%fused_computation.92 | convolution fusion | flops 301989888 | bytes 3670016 | tf_op jit(solution)/shard_map/dot_general | solution.py:100
  70.2 6.9 %all_gather.18 = bf16[512,128]{0,1:T(8,128)(2,1)S(1)} all-gather(bf16[256,128]{0,1:T(8,128)(2,1)S(1)} %get-tuple-element.13), channel_id=1, replica_groups=mesh['tenant'=2,'ctx'=2,'head'=8] {'ctx'}, dimensions={0}, use_global_device_ids=true | all-gather | bytes 196608 | tf_op jit(solution)/shard_map/all_gather | solution.py:134
  77.1 1.0 convolution_multiply_fusion.2
  78.1 1.9 %fusion.5 = bf16[256,128]{0,1:T(8,128)(2,1)S(1)} fusion(f32[256,128]{0,1:T(8,128)S(1)} %convolution_multiply_fusion.2, bf16[256,4608]{0,1:T(8,128)(2,1)S(1)} %bitcast.84, bf16[4608,128]{1,0:T(8,128)(2,1)} %all-gather.4.cloned.1.call-done), kind=kOutput, calls=%fused_computation.12 | convolution fusion | flops 302055424 | bytes 3735552 | tf_op jit(solution)/shard_map/dot_general | solution.py:100
  80.0 6.5 %all_gather.16 = bf16[512,128]{0,1:T(8,128)(2,1)S(1)} all-gather(bf16[256,128]{0,1:T(8,128)(2,1)S(1)} %fusion.5), channel_id=1, replica_groups=mesh['tenant'=2,'ctx'=2,'head'=8] {'ctx'}, dimensions={0}, use_global_device_ids=true | all-gather | bytes 196608 | tf_op jit(solution)/shard_map/all_gather | solution.py:135
  86.5 1.7 %convolution_multiply_fusion.1 = f32[256,256]{0,1:T(8,128)} fusion(bf16[16,256]{1,0:T(8,128)(2,1)S(1)} %copy-done.7, bf16[256,4608]{0,1:T(8,128)(2,1)S(1)} %bitcast.85, bf16[4608,16]{0,1:T(8,128)(2,1)S(1)} %copy-done), kind=kOutput, calls=%fused_computation.9 | convolution fusion | flops 39915520 | bytes 2777088 | tf_op jit(solution)/shard_map/dot_general | solution.py:113
  88.2 10.3 %all-gather.8.cloned.1.call-done = bf16[4608,256]{1,0:T(8,128)(2,1)} async-done(((bf16[2304,256]{1,0:T(8,128)(2,1)}), bf16[4608,256]{1,0:T(8,128)(2,1)}) %all-gather.8.cloned.1.call-update) | async-done | bytes 2359312 | tf_op jit(solution)/shard_map/all_gather | solution.py:102
  98.5 2.7 %convolution_add_fusion = f32[256,256]{0,1:T(8,128)S(1)} fusion(f32[256,256]{0,1:T(8,128)} %convolution_multiply_fusion.1, bf16[256,4608]{0,1:T(8,128)(2,1)S(1)} %bitcast.86, bf16[4608,256]{1,0:T(8,128)(2,1)} %all-gather.8.cloned.1.call-done), kind=kOutput, calls=%fused_computation.8 | convolution fusion | flops 604045312 | bytes 5242880 | tf_op jit(solution)/shard_map/dot_general | solution.py:100
  101.3 0.5 fusion.31
  101.8 0.2 fusion.7
  102.1 0.8 copy.19
  (53 shorter events, 0.7 us)
Async XLA Ops:
  6.5 80.0 %copy-start = (bf16[4608,16]{0,1:T(8,128)(2,1)S(1)}, bf16[4608,16]{0,1:T(8,128)(2,1)}, u32[]{:S(2)}) copy-start(bf16[4608,16]{0,1:T(8,128)(2,1)} %param.15) | copy-start | bytes 442372
  6.5 26.6 %copy-start.2 = (bf16[256,576]{0,1:T(8,128)(2,1)S(1)}, bf16[256,576]{0,1:T(8,128)(2,1)}, u32[]{:S(2)}) copy-start(bf16[256,576]{0,1:T(8,128)(2,1)} %param.11) | copy-start | bytes 884740
  6.5 2.2 %copy-start.3 = (s32[12]{0:T(128)S(1)}, s32[12]{0:T(128)}, u32[]{:S(2)}) copy-start(s32[12]{0:T(128)} %param.20) | copy-start | bytes 148
  6.5 2.3 %copy-start.4 = (s32[4]{0:T(128)S(1)}, s32[4]{0:T(128)}, u32[]{:S(2)}) copy-start(s32[4]{0:T(128)} %param.19) | copy-start | bytes 52
  6.5 2.8 %copy-start.5 = (s32[12]{0:T(128)S(1)}, s32[12]{0:T(128)}, u32[]{:S(2)}) copy-start(s32[12]{0:T(128)} %param.21) | copy-start | bytes 148
  6.5 60.5 %all-gather.6.cloned.1.call-start = ((), (), s32[]{:S(2)}) async-start(), calls=%async_computation.1 | async-start | bytes 1769472 | tf_op jit(solution)/shard_map/all_gather | solution.py:103
  7.3 70.8 %all-gather.4.cloned.1.call-start = ((), (), s32[]{:S(2)}) async-start(), calls=%async_computation | async-start | bytes 1769472 | tf_op jit(solution)/shard_map/all_gather | solution.py:104
  8.0 90.4 %all-gather.8.cloned.1.call-start = ((), (), s32[]{:S(2)}) async-start(), calls=%async_computation.2 | async-start | bytes 3538944 | tf_op jit(solution)/shard_map/all_gather | solution.py:102
  8.1 9.2 %collective-permute-start = (bf16[256,576]{0,1:T(8,128)(2,1)}, bf16[256,576]{0,1:T(8,128)(2,1)S(1)}, u32[]{:S(2)}, u32[]{:S(2)}) collective-permute-start(bf16[256,576]{0,1:T(8,128)(2,1)} %param.11), channel_id=1, source_target_pairs={{0,1},{1,2},{2,3},{3,4},{4,5},{5,6},{6,7},{7,0},{8,9},{9,10},{10,1... | collective-permute-start | bytes 884744 | tf_op jit(solution)/shard_map/ppermute | solution.py:27
  17.3 7.9 %collective-permute-start.1 = (bf16[256,576]{0,1:T(8,128)(2,1)S(1)}, bf16[256,576]{0,1:T(8,128)(2,1)S(1)}, u32[]{:S(2)}, u32[]{:S(2)}) collective-permute-start(bf16[256,576]{0,1:T(8,128)(2,1)S(1)} %collective-permute-done), channel_id=1, source_target_pairs={{0,1},{1,2},{2,3},{3,4},{4,5},{5,6},{6,7},{7,0},{8,9},{9,10},{10,1... | collective-permute-start | bytes 884744 | tf_op jit(solution)/shard_map/ppermute | solution.py:27
  25.2 7.9 %collective-permute-start.2 = (bf16[256,576]{0,1:T(8,128)(2,1)S(1)}, bf16[256,576]{0,1:T(8,128)(2,1)S(1)}, u32[]{:S(2)}, u32[]{:S(2)}) collective-permute-start(bf16[256,576]{0,1:T(8,128)(2,1)S(1)} %collective-permute-done.1), channel_id=1, source_target_pairs={{0,1},{1,2},{2,3},{3,4},{4,5},{5,6},{6,7},{7,0},{8,9},{9,10},{10,1... | collective-permute-start | bytes 884744 | tf_op jit(solution)/shard_map/ppermute | solution.py:27
  33.2 7.9 %collective-permute-start.3 = (bf16[256,576]{0,1:T(8,128)(2,1)S(1)}, bf16[256,576]{0,1:T(8,128)(2,1)S(1)}, u32[]{:S(2)}, u32[]{:S(2)}) collective-permute-start(bf16[256,576]{0,1:T(8,128)(2,1)S(1)} %collective-permute-done.2), channel_id=1, source_target_pairs={{0,1},{1,2},{2,3},{3,4},{4,5},{5,6},{6,7},{7,0},{8,9},{9,10},{10,1... | collective-permute-start | bytes 884744 | tf_op jit(solution)/shard_map/ppermute | solution.py:27
  41.1 7.9 %collective-permute-start.4 = (bf16[256,576]{0,1:T(8,128)(2,1)S(1)}, bf16[256,576]{0,1:T(8,128)(2,1)S(1)}, u32[]{:S(2)}, u32[]{:S(2)}) collective-permute-start(bf16[256,576]{0,1:T(8,128)(2,1)S(1)} %collective-permute-done.3), channel_id=1, source_target_pairs={{0,1},{1,2},{2,3},{3,4},{4,5},{5,6},{6,7},{7,0},{8,9},{9,10},{10,1... | collective-permute-start | bytes 884744 | tf_op jit(solution)/shard_map/ppermute | solution.py:27
  49.1 7.9 %collective-permute-start.5 = (bf16[256,576]{0,1:T(8,128)(2,1)S(1)}, bf16[256,576]{0,1:T(8,128)(2,1)S(1)}, u32[]{:S(2)}, u32[]{:S(2)}) collective-permute-start(bf16[256,576]{0,1:T(8,128)(2,1)S(1)} %collective-permute-done.4), channel_id=1, source_target_pairs={{0,1},{1,2},{2,3},{3,4},{4,5},{5,6},{6,7},{7,0},{8,9},{9,10},{10,1... | collective-permute-start | bytes 884744 | tf_op jit(solution)/shard_map/ppermute | solution.py:27
  57.0 7.9 %collective-permute-start.6 = (bf16[256,576]{0,1:T(8,128)(2,1)S(1)}, bf16[256,576]{0,1:T(8,128)(2,1)S(1)}, u32[]{:S(2)}, u32[]{:S(2)}) collective-permute-start(bf16[256,576]{0,1:T(8,128)(2,1)S(1)} %collective-permute-done.5), channel_id=1, source_target_pairs={{0,1},{1,2},{2,3},{3,4},{4,5},{5,6},{6,7},{7,0},{8,9},{9,10},{10,1... | collective-permute-start | bytes 884744 | tf_op jit(solution)/shard_map/ppermute | solution.py:27
  67.1 10.0 %copy-start.1 = (bf16[8,256,576]{1,2,0:T(8,128)(2,1)S(1)}, bf16[8,256,576]{1,2,0:T(8,128)(2,1)}, u32[]{:S(2)}) copy-start(bf16[8,256,576]{1,2,0:T(8,128)(2,1)} %gather_fusion) | copy-start | bytes 7077892
  67.1 10.0 %copy-start.6 = (bf16[4608,16]{0,1:T(8,128)(2,1)S(1)}, bf16[4608,16]{0,1:T(8,128)(2,1)}, u32[]{:S(2)}) copy-start(bf16[4608,16]{0,1:T(8,128)(2,1)} %param.17) | copy-start | bytes 442372
  67.1 10.0 %copy-start.8 = (bf16[16,128]{1,0:T(8,128)(2,1)S(1)}, bf16[16,128]{1,0:T(8,128)(2,1)}, u32[]{:S(2)}) copy-start(bf16[16,128]{1,0:T(8,128)(2,1)} %param.18) | copy-start | bytes 12292
  78.1 8.4 %copy-start.7 = (bf16[16,256]{1,0:T(8,128)(2,1)S(1)}, bf16[16,256]{1,0:T(8,128)(2,1)}, u32[]{:S(2)}) copy-start(bf16[16,256]{1,0:T(8,128)(2,1)} %param.16) | copy-start | bytes 24580
Sparse Core Ops, SparseCore 0:
  8.9 25.4 all-gather.5
  35.9 22.7 all-gather.3
  60.3 38.1 all-gather.7
